TPU v7x, 32 devices: a whole 2x2x4 slice. The times are simulated.
32 devices in a mesh: lat: 16 (over z, y, x), head: 2 (over core).
Axes of the slice: x: 2, y: 2, z: 4, core: 2. Of those that a mesh axis runs over, the one named last changes fastest.
Arguments:
- grid_latent: bfloat16 [131072, 512], P('lat'), may hold values from -6 to 6
- mesh_latent: bfloat16 [10240, 512], P('lat'), may hold values from -6 to 6
- neighbours: int32 [10240, 16], P('lat'), may hold values from -1 to 131071, as said below
- edge_bias: bfloat16 [10240, 64], P('lat', 'head'), may hold values from -8 to 384
- query_weight: bfloat16 [512, 512], P(None, 'head'), may hold values from -0.25 to 0.25
- key_weight: bfloat16 [512, 512], P(None, 'head'), may hold values from -0.25 to 0.25
- value_weight: bfloat16 [512, 512], P(None, 'head'), may hold values from -0.25 to 0.25
- out_weight: bfloat16 [512, 512], P('head'), may hold values from -0.25 to 0.25
- norm_gain: bfloat16 [512], P('head'), may hold values from 0.5 to 1.5
Outputs:
- mesh_out: bfloat16 [10240, 512], P('lat', 'head')
Inputs may be any that keep to these rules, and one draw needn't show every extreme that they name: `neighbours`: every neighbour of mesh node m is -1 or lies in [b * 8192 - 2048, (b + 1) * 8192 + 2048) with b = m // 640; both ends of that range (cut to the grid) are named in every draw; slots 0 and 1 are never -1.
All inputs are finite; a program needn't handle non-finite values.
Results may differ from a plain program's by a relative error of at most 0.0075.
Values may be sent and summed in bfloat16 or wider, within the bound.
A program may use at most 128 MiB of HBM per device.

v0:
```python
import functools

import jax
import jax.numpy as jnp
from jax import lax
from jax.experimental import pallas as pl
from jax.experimental.pallas import tpu as pltpu
from jax.sharding import PartitionSpec as P

HEAD_DIM = 128
LANES = 128
SUB = 8
EPSILON = 1e-05
DEAD = -1e30
PIECE = 1024
GROUP = 8
MESH = pl.DeviceIdType.MESH

WEIGHTS = 0
OWN_BIAS = 5
REQUEST = 6
REQUEST_COPIES = 4


def body(
    order_own, order_send, bias_send, grid_in, mesh_in, query_in, key_in, value_in, out_in, gain_in,
    out_ref,
    wide, stage, picked, query_w, key_w, value_w, out_w, gain,
    nodes, order_land, order_low, order_high, bias_land, bias_rows,
    fold, fold_own, mixed, mixed_own, lse, lse_own,
    partial, partial_lse, reply, reply_lse, normed,
    stage_sems, local_sems, order_sems, send_sems, recv_sems,
):
    band, width = grid_in.shape
    part = nodes.shape[1]
    heads = width // HEAD_DIM
    split = heads // 2
    cols = width // LANES
    side = width // 2
    chunks = order_own.shape[0]
    chunk_rows = LANES * cols
    padded = lse.shape[1]
    reply_base = REQUEST + 2 * REQUEST_COPIES
    last_copy = reply_base + 2 * (heads + 1)

    lat = lax.axis_index("lat")
    me = lax.axis_index("head")
    size = lax.axis_size("lat")
    other = 1 - me
    above = lax.rem(lat + 1, size)
    below = lax.rem(lat + size - 1, size)
    partner = (lat, other)

    def fetch(n):
        return pltpu.make_async_copy(
            grid_in.at[pl.ds(n * PIECE, PIECE)], stage.at[n % 2], stage_sems.at[n % 2]
        )

    fetch(0).start()
    fetch(1).start()
    mine = [
        pltpu.make_async_copy(src, dst, local_sems.at[n])
        for n, (src, dst) in enumerate((
            (query_in, query_w.at[me]),
            (key_in, key_w.at[me]),
            (value_in, value_w.at[me]),
            (out_in, out_w.at[pl.ds(me * side, side)]),
            (gain_in, gain.at[me]),
            (bias_send.at[2, me], bias_land.at[2, me]),
            (mesh_in.at[pl.ds(me * part, part)], nodes.at[2]),
        ))
    ]
    for copy in mine:
        copy.start()

    barrier = pltpu.get_barrier_semaphore()
    peers = (partner, (above, me), (below, me), (above, other), (below, other))
    for peer in peers:
        pl.semaphore_signal(barrier, inc=1, device_id=peer, device_id_type=MESH)
    pl.semaphore_wait(barrier, len(peers))

    def remote(n, src, dst, device):
        return pltpu.make_async_remote_copy(
            src_ref=src, dst_ref=dst, send_sem=send_sems.at[n], recv_sem=recv_sems.at[n],
            device_id=device, device_id_type=MESH,
        )

    requests = []
    for s, target in enumerate((above, below)):
        at = REQUEST + s * REQUEST_COPIES
        requests.append((
            remote(at, order_send.at[s], order_land.at[s], (target, me)),
            remote(at + 1, bias_send.at[s, me], bias_land.at[s, me], (target, me)),
            remote(at + 2, bias_send.at[s, other], bias_land.at[s, me], (target, other)),
            remote(at + 3, mesh_in.at[pl.ds(me * part, part)], nodes.at[s], (target, me)),
        ))
    shared = [
        remote(WEIGHTS, query_in, query_w.at[me], partner),
        remote(WEIGHTS + 1, key_in, key_w.at[me], partner),
        remote(WEIGHTS + 2, value_in, value_w.at[me], partner),
        remote(WEIGHTS + 3, out_in, out_w.at[pl.ds(me * side, side)], partner),
        remote(WEIGHTS + 4, gain_in, gain.at[me], partner),
        remote(OWN_BIAS, bias_send.at[2, other], bias_land.at[2, me], partner),
    ]
    for copy in requests[0]:
        copy.start()
    for copy in shared:
        copy.start()
    for copy in requests[1]:
        copy.start()

    lse[...] = jnp.zeros(lse.shape, jnp.float32)

    pieces = band // PIECE
    for n in range(pieces):
        fetch(n).wait()

        def widen(step, carry, n=n):
            row = pl.multiple_of(step * 32, 32)
            block = stage[n % 2, pl.ds(row, 32), :].astype(jnp.float32)
            for t in range(4):
                for c in range(cols):
                    at = n * PIECE * cols + row * cols + (t * cols + c) * SUB
                    wide[pl.ds(pl.multiple_of(at, SUB), SUB), :] = block[
                        t * SUB : (t + 1) * SUB, c * LANES : (c + 1) * LANES
                    ]
            return carry

        lax.fori_loop(0, PIECE // 32, widen, 0)
        if n + 2 < pieces:
            fetch(n + 2).start()

    diagonal = (
        lax.broadcasted_iota(jnp.int32, (SUB, LANES), 1) // (LANES // SUB)
        == lax.broadcasted_iota(jnp.int32, (SUB, LANES), 0)
    )
    lane = lax.broadcasted_iota(jnp.int32, (padded, LANES), 1)

    def project(s, fold_ref):
        rows = nodes[s]
        for half in range(2):
            queries = jnp.dot(
                rows, query_w[half], preferred_element_type=jnp.float32
            ).astype(jnp.bfloat16)
            for h in range(split):
                span = slice(h * HEAD_DIM, (h + 1) * HEAD_DIM)
                fold_ref[half * split + h] = lax.dot_general(
                    queries[:, span], key_w[half, :, span],
                    (((1,), (1,)), ((), ())), preferred_element_type=jnp.float32,
                )
        bias_rows[...] = jnp.concatenate(
            [bias_land[s, half].astype(jnp.float32) for half in range(2)], axis=0
        )

    def gather(order, chunk, u):
        for e in range(LANES):
            at = order[chunk, e]
            to = u * chunk_rows + (e // SUB) * (cols * SUB) + e % SUB
            picked[pl.ds(to, cols, stride=SUB), :] = wide[pl.ds(at, cols, stride=SUB), :]

    def score(fold_ref, mixed_ref, lse_ref, chunk, u):
        start = u * chunk_rows
        rows = jnp.concatenate(
            [
                jnp.concatenate(
                    [
                        picked[start + (t * cols + c) * SUB : start + (t * cols + c + 1) * SUB, :]
                        for t in range(LANES // SUB)
                    ],
                    axis=0,
                ).astype(jnp.bfloat16)
                for c in range(cols)
            ],
            axis=1,
        )
        at = pl.ds(pl.multiple_of(chunk * SUB, SUB), SUB)
        left = jnp.concatenate([fold_ref[h, at, :] for h in range(heads)], axis=0)
        scores = lax.dot_general(
            left.astype(jnp.bfloat16), rows,
            (((1,), (1,)), ((), ())), preferred_element_type=jnp.float32,
        )
        bias = jnp.concatenate(
            [
                jnp.where(diagonal, bias_rows[pl.ds(h * chunks + chunk, 1), :], DEAD)
                for h in range(heads)
            ],
            axis=0,
        )
        scores = scores * HEAD_DIM ** (-0.5) + bias
        top = jnp.max(scores, axis=1, keepdims=True)
        weights = jnp.exp(scores - top)
        total = jnp.sum(weights, axis=1, keepdims=True)
        summed = jnp.dot(
            weights.astype(jnp.bfloat16), rows, preferred_element_type=jnp.float32
        ) * (1.0 / total)
        level = jnp.broadcast_to(top + jnp.log(total), (heads * SUB, LANES))
        for h in range(heads):
            mixed_ref[h, at, :] = summed[h * SUB : (h + 1) * SUB]
            lse_ref[h, at, :] = level[h * SUB : (h + 1) * SUB]

    def run(order, fold_ref, mixed_ref, lse_ref, low, high):
        for u in range(GROUP):
            gather(order, low + u, u)

        def step(n, carry):
            chunk = low + n * GROUP
            after = lax.rem(chunk + GROUP, chunks)
            for u in range(GROUP):
                score(fold_ref, mixed_ref, lse_ref, chunk + u, u)
            for u in range(GROUP):
                gather(order, after + u, u)
            return carry

        lax.fori_loop(0, (high - low) // GROUP, step, 0)

    def values(mixed_ref, h):
        half, inner = h // split, h % split
        return jnp.dot(
            mixed_ref[h].astype(jnp.bfloat16),
            value_w[half, :, inner * HEAD_DIM : (inner + 1) * HEAD_DIM],
            preferred_element_type=jnp.float32,
        )

    for copy in mine:
        copy.wait()
    for copy in shared:
        copy.wait_recv()
    project(2, fold_own)
    first = (chunks // GROUP // 2) * GROUP
    run(order_own, fold_own, mixed_own, lse_own, 0, first)

    replies = []
    for s, (target, order) in enumerate(((below, order_low), (above, order_high))):
        order_copy = pltpu.make_async_copy(order_land.at[s], order, order_sems.at[s])
        requests[s][0].wait_recv()
        order_copy.start()
        for copy in requests[s][1:]:
            copy.wait_recv()
        project(s, fold)
        order_copy.wait()
        run(order, fold, mixed, lse, 0, chunks)
        sends = [
            remote(reply_base + s * (heads + 1) + h, partial.at[s, h], reply.at[s, h], (target, me))
            for h in range(heads)
        ] + [
            remote(
                reply_base + s * (heads + 1) + heads, partial_lse.at[s], reply_lse.at[s],
                (target, me),
            )
        ]
        level = lse[0]
        for h in range(1, heads):
            level = jnp.where(lane == h, lse[h], level)
        for b in range(padded // LANES):
            partial_lse[s, :, b * LANES : (b + 1) * LANES] = level[
                b * LANES : (b + 1) * LANES
            ].T[:SUB]
        for h in range(heads):
            partial[s, h] = values(mixed, h).astype(jnp.bfloat16)
            if h == 0:
                sends[heads].start()
            else:
                sends[h - 1].start()
        sends[heads - 1].start()
        replies.append(sends)

    project_bias = jnp.concatenate(
        [bias_land[2, half].astype(jnp.float32) for half in range(2)], axis=0
    )
    bias_rows[...] = project_bias
    run(order_own, fold_own, mixed_own, lse_own, first, chunks)

    for sends in replies:
        for copy in sends:
            copy.wait_recv()
    filler = jnp.zeros((LANES - SUB, LANES), jnp.float32)
    levels = [
        jnp.concatenate(
            [
                jnp.concatenate(
                    [reply_lse[s, :, b * LANES : (b + 1) * LANES], filler], axis=0
                ).T
                for b in range(padded // LANES)
            ],
            axis=0,
        )[:part]
        for s in range(2)
    ]
    attended = []
    for h in range(heads):
        low, high = levels[0][:, h : h + 1], levels[1][:, h : h + 1]
        own = lse_own[h, :part, :]
        top = jnp.maximum(own, jnp.maximum(low, high))
        share_low, share_high = jnp.exp(low - top), jnp.exp(high - top)
        share_own = jnp.exp(own - top)
        total = share_low + share_high + share_own
        summed = (
            share_own * values(mixed_own, h)
            + share_low * reply[0, h].astype(jnp.float32)
            + share_high * reply[1, h].astype(jnp.float32)
        )
        attended.append((summed * (1.0 / total)).astype(jnp.bfloat16))
    updated = nodes[2].astype(jnp.float32) + jnp.dot(
        jnp.concatenate(attended, axis=1), out_w[...], preferred_element_type=jnp.float32
    )
    mean = jnp.sum(updated, axis=1, keepdims=True) / width
    variance = jnp.sum(updated * updated, axis=1, keepdims=True) / width - mean * mean
    result = (updated - mean) * lax.rsqrt(variance + EPSILON)
    for half in range(2):
        normed[half] = (
            result[:, half * side : (half + 1) * side] * gain[half, :1, :]
        ).astype(jnp.bfloat16)

    here = out_ref.at[pl.ds(me * part, part)]
    give = remote(last_copy, normed.at[other], here, partner)
    keep = pltpu.make_async_copy(normed.at[me], here, local_sems.at[0])
    give.start()
    keep.start()
    for group in requests:
        for copy in group:
            copy.wait_send()
    for copy in shared:
        copy.wait_send()
    for sends in replies:
        for copy in sends:
            copy.wait_send()
    keep.wait()
    give.wait()


def shards(
    grid_latent,
    mesh_latent,
    neighbours,
    edge_bias,
    query_weight,
    key_weight,
    value_weight,
    out_weight,
    norm_gain,
):
    band, width = grid_latent.shape
    count, slots = neighbours.shape
    part = count // 2
    cols = width // LANES
    heads = width // HEAD_DIM
    split = heads // 2
    side = width // 2
    per_chunk = LANES // slots
    chunks = part // per_chunk
    padded = -(-part // LANES) * LANES
    me = lax.axis_index("head")
    lat = lax.axis_index("lat")
    size = lax.axis_size("lat")

    flat = neighbours.reshape(2 * chunks, LANES)
    dests = (lax.rem(lat + 1, size), lax.rem(lat + size - 1, size), lat)
    bias = edge_bias.reshape(2, chunks, per_chunk, split, slots).transpose(0, 3, 1, 2, 4)
    bias = bias.reshape(2, split, chunks, LANES)
    orders, biases = [], []
    for dest in dests:
        local = flat - dest * band
        inside = (local >= 0) & (local < band)
        row = jnp.where(inside, local, 0)
        address = (row // SUB) * (SUB * cols) + row % SUB
        orders.append(lax.dynamic_slice_in_dim(address, me * chunks, chunks, 0))
        biases.append(
            jnp.where(inside.reshape(2, 1, chunks, LANES), bias, DEAD)
            .astype(jnp.bfloat16)
            .reshape(2, split * chunks, LANES)
        )
    order_send = jnp.stack(orders[:2])
    bias_send = jnp.stack(biases)
    gain = jnp.broadcast_to(norm_gain.astype(jnp.float32)[None, :], (SUB, side))

    smem = pl.BlockSpec(memory_space=pltpu.SMEM)
    far = pl.BlockSpec(memory_space=pltpu.HBM)
    copies = REQUEST + 2 * REQUEST_COPIES + 2 * (heads + 1) + 1
    bf16, f32 = jnp.bfloat16, jnp.float32
    return pl.pallas_call(
        body,
        name="attend",
        out_shape=jax.ShapeDtypeStruct((count, side), bf16),
        in_specs=[smem] + [far] * 9,
        out_specs=far,
        scratch_shapes=[
            pltpu.VMEM((band * cols, LANES), f32),
            pltpu.VMEM((2, PIECE, width), bf16),
            pltpu.VMEM((GROUP * LANES * cols, LANES), f32),
            pltpu.VMEM((2, width, side), bf16),
            pltpu.VMEM((2, width, side), bf16),
            pltpu.VMEM((2, width, side), bf16),
            pltpu.VMEM((width, width), bf16),
            pltpu.VMEM((2, SUB, side), f32),
            pltpu.VMEM((3, part, width), bf16),
            pltpu.VMEM((2, chunks, LANES), jnp.int32),
            pltpu.SMEM((chunks, LANES), jnp.int32),
            pltpu.SMEM((chunks, LANES), jnp.int32),
            pltpu.VMEM((3, 2, split * chunks, LANES), bf16),
            pltpu.VMEM((heads * chunks, LANES), f32),
            pltpu.VMEM((heads, part, width), f32),
            pltpu.VMEM((heads, part, width), f32),
            pltpu.VMEM((heads, part, width), f32),
            pltpu.VMEM((heads, part, width), f32),
            pltpu.VMEM((heads, padded, LANES), f32),
            pltpu.VMEM((heads, padded, LANES), f32),
            pltpu.VMEM((2, heads, part, HEAD_DIM), bf16),
            pltpu.VMEM((2, SUB, padded), f32),
            pltpu.VMEM((2, heads, part, HEAD_DIM), bf16),
            pltpu.VMEM((2, SUB, padded), f32),
            pltpu.VMEM((2, part, side), bf16),
            pltpu.SemaphoreType.DMA((2,)),
            pltpu.SemaphoreType.DMA((7,)),
            pltpu.SemaphoreType.DMA((2,)),
            pltpu.SemaphoreType.DMA((copies,)),
            pltpu.SemaphoreType.DMA((copies,)),
        ],
        compiler_params=pltpu.CompilerParams(
            collective_id=0, has_side_effects=True, vmem_limit_bytes=56 * 1024 * 1024
        ),
    )(
        orders[2], order_send, bias_send, grid_latent, mesh_latent,
        query_weight, key_weight, value_weight, out_weight, gain,
    )


def solution(mesh):
    in_specs = (
        P("lat", None),
        P("lat", None),
        P("lat", None),
        P("lat", "head"),
        P(None, "head"),
        P(None, "head"),
        P(None, "head"),
        P("head", None),
        P("head"),
    )
    out_specs = P("lat", "head")
    return jax.shard_map(shards, mesh=mesh, in_specs=in_specs, out_specs=out_specs, check_vma=False)
```

profile of v0, /device:TPU:5, one launch (start us, length us, event | category | flops | bytes accessed | tf_op | source)
XLA Modules:
  0.0 75.6 jit_solution(1677015591648677731)
XLA Ops:
  0.0 0.8 %compare_and_fusion.2 = (pred[640,16]{0,1:T(8,128)(4,1)S(1)}, s32[640,16]{0,1:T(8,128)S(1)}, pred[640,16]{0,1:T(8,128)(4,1)S(1)}, s32[640,16]{0,1:T(8,128)S(1)},...) fusion(s32[640,16]{0,1:T(8,128)} %param.11, s32[]{:T(128)S(6)} %mul.26, s32[]{:T(128)S(6)} %mul.23, s32[]{:T(128)S(6)} %mul.28), kind=kLoop, calls=%fused_computation.7 | loop fusion | flops 122880 | bytes 194572 | tf_op jit(solution)/shard_map/and | solution.py:363
  0.8 0.2 copy.14
  1.0 0.1 sub.61
  1.2 0.6 fusion.7.order_own
  1.8 0.2 copy.15
  2.0 0.1 sub.65
  2.2 0.2 copy.16
  2.4 0.1 sub.70
  2.6 0.6 pad_add_fusion.order_send
  3.2 0.2 copy.17
  3.5 0.2 and.76
  3.6 0.9 %copy.18 = bf16[640,32]{1,0:T(8,128)(2,1)S(1)} copy(bf16[640,32]{0,1:T(8,128)(2,1)} %param.12) | data formatting | bytes 81920 | tf_op args[3]
  4.6 0.2 reshape.119
  4.8 0.5 copy.19
  5.2 0.1 reshape.120
  5.3 0.1 copy.20
  5.4 0.2 copy.23
  5.7 0.2 and.80
  5.9 0.2 copy.21
  6.1 0.2 and.78
  6.3 0.7 pad_maximum_fusion.bias_send
  7.0 1.2 %broadcast_in_dim.47.gain_in = f32[8,256]{1,0:T(8,128)} broadcast(bf16[256]{0:T(256)(128)(2,1)} %param.17), dimensions={1} | broadcast | bytes 8704 | tf_op jit(solution)/shard_map/broadcast_in_dim | solution.py:374
  8.2 65.7 %attend.1 = bf16[640,256]{1,0:T(8,128)(2,1)} custom-call(s32[40,128]{1,0:T(8,128)} %fusion.7.order_own, s32[2,40,128]{2,1,0:T(8,128)} %pad_add_fusion.order_send, bf16[3,2,80,128]{3,2,1,0:T(8,128)(2,1)} %pad_maximum_fusion.bias_send, bf16[8192,512]{1,0:T(8,128)(2,1)} %grid_in.1, bf16[640,512]{1,0:T(8,128)(2,1)} %mesh_in.1, bf16[512,256]{1,0:T(8,128)(2,1)} %query_in.1, ...), custom_call_target="tpu_custom_call" | custom-call | tf_op jit(solution)/shard_map/attend/pallas_call | solution.py:380
  73.9 1.7 %copy.26 = bf16[640,256]{1,0:T(8,128)(2,1)} copy(bf16[640,256]{1,0:T(8,128)(2,1)} %attend.1) | data formatting | bytes 655360
  (11 shorter events, 0.2 us)
where the time goes:
time: 76.1 us; the launch traced here: 75.6 us
  Pallas kernels  65.7 us (86%)
  local copies, waits for them, and re-layouts  6.86 us (9%)
  other arithmetic  2.9 us (4%)
    pallas_call x1, Pallas kernels, shards(): pl.pallas_call(body, name='attend', out_shape=jax.ShapeDtypeStruct((count...  65.7 us
    unnamed x2, local copies, waits for them, and re-layouts  2.66 us

commit v1 on v0

v1 whole, which is shorter than its diff:
```python
import functools

import jax
import jax.numpy as jnp
from jax import lax
from jax.experimental import pallas as pl
from jax.experimental.pallas import tpu as pltpu
from jax.sharding import PartitionSpec as P

HEAD_DIM = 128
LANES = 128
SUB = 8
EPSILON = 1e-05
DEAD = -1e30
PIECE = 1024
HALVES = 2
GROUP = 5
MIX = 10
MESH = pl.DeviceIdType.MESH

SHARED = 0
REQUEST = 6
REQUEST_COPIES = 4
REPLY = REQUEST + 2 * REQUEST_COPIES


def body(
    grid_in, mesh_in, neigh_in, bias_in, query_in, key_in, value_in, out_in, gain_in,
    out_ref,
    wide, stage, picked, rows, query_w, key_w, value_w, out_w, gain_mine, gain_theirs,
    neigh, bias, order_send, bias_send, nodes, order_land, order_own, order_low, order_high,
    bias_land, bias_rows, bias_own, fold, fold_own, scores, weights, mixed, lse,
    mixed_own, lse_own, partial, partial_lse, reply, reply_lse, normed,
    stage_sems, local_sems, order_sems, send_sems, recv_sems,
):
    band, width = grid_in.shape
    part = nodes.shape[1]
    slots, count = neigh.shape
    per_chunk = LANES // slots
    heads = width // HEAD_DIM
    split = heads // 2
    cols = width // LANES
    side = width // 2
    chunks = order_own.shape[0]
    chunk_rows = LANES * cols
    left_rows = heads * SUB
    padded = lse.shape[1]
    piece = part // HALVES
    piece_chunks = chunks // HALVES
    bf16, f32 = jnp.bfloat16, jnp.float32

    lat = lax.axis_index("lat")
    me = lax.axis_index("head")
    size = lax.axis_size("lat")
    other = 1 - me
    partner = (lat, other)
    sides = (
        (lat + 1, lat < size - 1, lat - 1, lat > 0),
        (lat - 1, lat > 0, lat + 1, lat < size - 1),
    )

    def fetch(n):
        return pltpu.make_async_copy(
            grid_in.at[pl.ds(n * PIECE, PIECE)], stage.at[n % 2], stage_sems.at[n % 2]
        )

    mine = [
        pltpu.make_async_copy(src, dst, local_sems.at[n])
        for n, (src, dst) in enumerate((
            (neigh_in, neigh),
            (bias_in, bias),
            (query_in, query_w.at[me]),
            (key_in, key_w.at[me]),
            (value_in, value_w.at[me]),
            (out_in, out_w.at[pl.ds(me * side, side)]),
            (gain_in, gain_mine),
            (mesh_in.at[pl.ds(me * part, part)], nodes.at[2]),
        ))
    ]
    for copy in mine:
        copy.start()
    fetch(0).start()
    fetch(1).start()

    barrier = pltpu.get_barrier_semaphore()

    def signal(device):
        pl.semaphore_signal(barrier, inc=1, device_id=device, device_id_type=MESH)

    signal(partner)
    for target, there, _, _ in sides:
        @pl.when(there)
        def _(target=target):
            signal((target, me))
            signal((target, other))
    pl.semaphore_wait(barrier, 1 + 2 * ((lat + size - 1) // size) + 2 * ((2 * size - 2 - lat) // size))

    def remote(n, src, dst, device):
        return pltpu.make_async_remote_copy(
            src_ref=src, dst_ref=dst, send_sem=send_sems.at[n], recv_sem=recv_sems.at[n],
            device_id=device, device_id_type=MESH,
        )

    def request(s):
        at, target = REQUEST + s * REQUEST_COPIES, sides[s][0]
        order = order_send.at[s, pl.ds(me * chunks, chunks)]
        return (
            remote(at, mesh_in.at[pl.ds(me * part, part)], nodes.at[s], (target, me)),
            remote(at + 1, order, order_land.at[s], (target, me)),
            remote(at + 2, bias_send.at[s, me], bias_land.at[s, me], (target, me)),
            remote(at + 3, bias_send.at[s, other], bias_land.at[s, me], (target, other)),
        )

    def answer(s, half):
        at, target = REPLY + (s * HALVES + half) * 2, sides[s][2]
        return (
            remote(at, partial_lse.at[s, half], reply_lse.at[s, half], (target, me)),
            remote(at + 1, partial.at[s, half], reply.at[s, half], (target, me)),
        )

    shared = [
        remote(SHARED, query_in, query_w.at[me], partner),
        remote(SHARED + 1, key_in, key_w.at[me], partner),
        remote(SHARED + 2, value_in, value_w.at[me], partner),
        remote(SHARED + 3, out_in, out_w.at[pl.ds(me * side, side)], partner),
        remote(SHARED + 4, gain_in, gain_theirs, partner),
        remote(SHARED + 5, bias_send.at[2, other], bias_land.at[2, me], partner),
    ]

    @pl.when(sides[0][1])
    def _():
        request(0)[0].start()

    for copy in shared[:5]:
        copy.start()

    mine[0].wait()
    mine[1].wait()
    index = neigh[...]
    away = jnp.where(index >= 0, index - (lat - 1) * band, 3 * band)
    fields = (
        jnp.right_shift(away, 8).astype(f32).astype(bf16),
        jnp.bitwise_and(away, 255).astype(f32).astype(bf16),
    )

    def iota(shape, axis):
        return lax.broadcasted_iota(jnp.int32, shape, axis)

    def as_mask(value):
        return jnp.where(value, 1.0, 0.0).astype(bf16)

    spread = as_mask(iota((slots, LANES), 0) == iota((slots, LANES), 1) % slots)
    shape = (split * slots, split * LANES)
    spread_bias = as_mask(
        (iota(shape, 0) // slots == iota(shape, 1) // LANES)
        & (iota(shape, 0) % slots == iota(shape, 1) % slots)
    )
    shape = (count, (2 + split) * LANES)
    laid = jnp.concatenate(
        [
            lax.dot_general(value, to, (((0,), (0,)), ((), ())), preferred_element_type=f32)
            for value, to in (*((field, spread) for field in fields), (bias[...], spread_bias))
        ],
        axis=1,
    )
    own_lane = iota(shape, 1) % LANES // slots == iota(shape, 0) % per_chunk
    laid = jnp.where(own_lane, laid, 0.0).astype(bf16)
    shape = (2 * chunks, count)
    gathered = jnp.dot(
        as_mask(iota(shape, 0) == iota(shape, 1) // per_chunk), laid, preferred_element_type=f32
    )
    away = (gathered[:, :LANES] * 256.0 + gathered[:, LANES : 2 * LANES]).astype(jnp.int32)
    for s, step in enumerate((2, 0, 1)):
        local = away - step * band
        inside = (local >= 0) & (local < band)
        row = jnp.where(inside, local, 0)
        order_send[s] = row * cols
        for h in range(split):
            at = (2 + h) * LANES
            masked = jnp.where(inside, gathered[:, at : at + LANES], DEAD).astype(bf16)
            for half in range(2):
                bias_send[s, half, h] = masked[half * chunks : (half + 1) * chunks]

    @pl.when(sides[0][1])
    def _():
        for copy in request(0)[1:]:
            copy.start()

    @pl.when(sides[1][1])
    def _():
        for copy in request(1):
            copy.start()

    shared[5].start()
    keep_bias = pltpu.make_async_copy(bias_send.at[2, me], bias_land.at[2, me], local_sems.at[0])
    keep_bias.start()
    keep_order = pltpu.make_async_copy(
        order_send.at[2, pl.ds(me * chunks, chunks)], order_own, order_sems.at[2]
    )
    keep_order.start()

    pieces = band // PIECE
    for n in range(pieces):
        fetch(n).wait()

        def widen(step, carry, n=n):
            row = pl.multiple_of(step * 32, 32)
            block = stage[n % 2, pl.ds(row, 32), :].astype(f32)
            for t in range(4):
                for c in range(cols):
                    at = (n * PIECE + row + t * SUB) * cols + c
                    wide[pl.ds(at, SUB, stride=cols), :] = block[
                        t * SUB : (t + 1) * SUB, c * LANES : (c + 1) * LANES
                    ]
            return carry

        lax.fori_loop(0, PIECE // 32, widen, 0)
        if n + 2 < pieces:
            fetch(n + 2).start()

    diagonal = iota((SUB, LANES), 1) // slots == iota((SUB, LANES), 0)
    lane = iota((padded, LANES), 1)

    def project(s, fold_ref, bias_ref):
        inputs = nodes[s]
        for half in range(2):
            queries = jnp.dot(inputs, query_w[half], preferred_element_type=f32).astype(bf16)
            for h in range(split):
                span = slice(h * HEAD_DIM, (h + 1) * HEAD_DIM)
                fold_ref[half * split + h] = lax.dot_general(
                    queries[:, span], key_w[half, :, span],
                    (((1,), (1,)), ((), ())), preferred_element_type=f32,
                )
                at = (half * split + h) * chunks
                bias_ref[at : at + chunks, :] = bias_land[s, half, h].astype(f32)

    def gather(order, chunk, u):
        line = order.at[chunk]
        for e in range(LANES):
            at = u * chunk_rows + e * cols
            picked[at : at + cols, :] = wide[pl.ds(line[e], cols), :]

    def block(chunk, size):
        return pl.ds(pl.multiple_of(chunk * size, size), size)

    def score(fold_ref, base, chunk, u):
        found = jnp.concatenate(
            [
                jnp.concatenate(
                    [
                        picked[pl.ds(u * chunk_rows + t * SUB * cols + c, SUB, stride=cols), :]
                        for t in range(LANES // SUB)
                    ],
                    axis=0,
                ).astype(bf16)
                for c in range(cols)
            ],
            axis=1,
        )
        rows[block(chunk, LANES), :] = found
        left = jnp.concatenate(
            [fold_ref[h, block(base + chunk, SUB), :] for h in range(heads)], axis=0
        )
        scores[block(chunk, left_rows), :] = lax.dot_general(
            left.astype(bf16), found, (((1,), (1,)), ((), ())), preferred_element_type=f32
        )

    def soften(bias_ref, lse_ref, base, chunk):
        here = jnp.concatenate(
            [
                jnp.where(diagonal, bias_ref[pl.ds(h * chunks + base + chunk, 1), :], DEAD)
                for h in range(heads)
            ],
            axis=0,
        )
        value = scores[block(chunk, left_rows), :] * HEAD_DIM ** (-0.5) + here
        top = jnp.max(value, axis=1, keepdims=True)
        grown = jnp.exp(value - top)
        total = jnp.sum(grown, axis=1, keepdims=True)
        weights[block(chunk, left_rows), :] = (grown * (1.0 / total)).astype(bf16)
        level = jnp.broadcast_to(top + jnp.log(total), (left_rows, LANES))
        for h in range(heads):
            lse_ref[h, block(chunk, SUB), :] = level[h * SUB : (h + 1) * SUB]

    def mix(mixed_ref, chunk):
        summed = jnp.dot(
            weights[block(chunk, left_rows), :], rows[block(chunk, LANES), :],
            preferred_element_type=f32,
        )
        for h in range(heads):
            mixed_ref[h, block(chunk, SUB), :] = summed[h * SUB : (h + 1) * SUB]

    def run(order, fold_ref, bias_ref, mixed_ref, lse_ref, half):
        base = half * piece_chunks
        for u in range(GROUP):
            gather(order, base + u, u)

        def scoring(n, carry):
            chunk = n * GROUP
            for u in range(GROUP):
                score(fold_ref, base, chunk + u, u)
            for u in range(GROUP):
                gather(order, base + chunk + GROUP + u, u)
            return carry

        lax.fori_loop(0, piece_chunks // GROUP - 1, scoring, 0)
        for u in range(GROUP):
            score(fold_ref, base, piece_chunks - GROUP + u, u)

        def softening(n, carry):
            for u in range(piece_chunks):
                soften(bias_ref, lse_ref, base, n * piece_chunks + u)
            return carry

        lax.fori_loop(0, 1, softening, 0)

        def mixing(n, carry):
            for u in range(MIX):
                mix(mixed_ref, n * MIX + u)
            return carry

        lax.fori_loop(0, piece_chunks // MIX, mixing, 0)

    def values(mixed_ref, h):
        half, inner = h // split, h % split
        return jnp.dot(
            mixed_ref[h].astype(bf16),
            value_w[half, :, inner * HEAD_DIM : (inner + 1) * HEAD_DIM],
            preferred_element_type=f32,
        )

    lse[...] = jnp.zeros(lse.shape, f32)
    for copy in mine[2:]:
        copy.wait()
    for copy in shared:
        copy.wait_recv()
    keep_bias.wait()
    keep_order.wait()

    project(2, fold_own, bias_own)
    run(order_own, fold_own, bias_own, mixed_own.at[0], lse_own.at[0], 0)

    for s, order in enumerate((order_low, order_high)):
        _, sent, _, received = sides[s]

        @pl.when(received)
        def _(s=s, order=order):
            needs = request(s)
            order_copy = pltpu.make_async_copy(order_land.at[s], order, order_sems.at[s])
            for copy in needs:
                copy.wait_recv()
            order_copy.start()
            order_copy.wait()
            project(s, fold, bias_rows)
            for half in range(HALVES):
                run(order, fold, bias_rows, mixed, lse, half)
                level = lse[0]
                for h in range(1, heads):
                    level = jnp.where(lane == h, lse[h], level)
                for b in range(padded // LANES):
                    span = slice(b * LANES, (b + 1) * LANES)
                    partial_lse[s, half, :, span] = level[span].T[:SUB]
                for h in range(heads):
                    partial[s, half, h] = values(mixed, h).astype(bf16)
                for copy in answer(s, half):
                    copy.start()

        @pl.when(jnp.logical_not(sent))
        def _(s=s):
            reply[s] = jnp.zeros(reply.shape[1:], bf16)
            reply_lse[s] = jnp.full(reply_lse.shape[1:], DEAD, f32)

    for half in range(1, HALVES):
        run(order_own, fold_own, bias_own, mixed_own.at[half], lse_own.at[half], half)

    filler = jnp.zeros((LANES - SUB, LANES), f32)
    gains = [
        jnp.where(me == side_of, gain_mine[...], gain_theirs[...]).reshape(1, side).astype(f32)
        for side_of in range(2)
    ]
    give, keep = [], []
    for half in range(HALVES):
        for s in range(2):
            @pl.when(sides[s][1])
            def _(s=s, half=half):
                for copy in answer(s, half):
                    copy.wait_recv()
        levels = [
            jnp.concatenate(
                [
                    jnp.concatenate(
                        [reply_lse[s, half, :, b * LANES : (b + 1) * LANES], filler], axis=0
                    ).T
                    for b in range(padded // LANES)
                ],
                axis=0,
            )[:piece]
            for s in range(2)
        ]
        attended = []
        for h in range(heads):
            low, high = levels[0][:, h : h + 1], levels[1][:, h : h + 1]
            own = lse_own[half, h]
            top = jnp.maximum(own, jnp.maximum(low, high))
            share_low, share_high = jnp.exp(low - top), jnp.exp(high - top)
            share_own = jnp.exp(own - top)
            total = share_low + share_high + share_own
            summed = (
                share_own * values(mixed_own.at[half], h)
                + share_low * reply[0, half, h].astype(f32)
                + share_high * reply[1, half, h].astype(f32)
            )
            attended.append((summed * (1.0 / total)).astype(bf16))
        updated = nodes[2, half * piece : (half + 1) * piece].astype(f32) + jnp.dot(
            jnp.concatenate(attended, axis=1), out_w[...], preferred_element_type=f32
        )
        mean = jnp.sum(updated, axis=1, keepdims=True) / width
        variance = jnp.sum(updated * updated, axis=1, keepdims=True) / width - mean * mean
        result = (updated - mean) * lax.rsqrt(variance + EPSILON)
        for b in range(2):
            normed[half, b] = (result[:, b * side : (b + 1) * side] * gains[b]).astype(bf16)
        here = out_ref.at[pl.ds(me * part + half * piece, piece)]
        at = REPLY + 4 * HALVES + half
        give.append(remote(at, normed.at[half, other], here, partner))
        keep.append(pltpu.make_async_copy(normed.at[half, me], here, local_sems.at[1 + half]))
        give[half].start()
        keep[half].start()

    for copy in shared:
        copy.wait_send()
    for s in range(2):
        @pl.when(sides[s][1])
        def _(s=s):
            for copy in request(s):
                copy.wait_send()

        @pl.when(sides[s][3])
        def _(s=s):
            for half in range(HALVES):
                for copy in answer(s, half):
                    copy.wait_send()
    for copy in keep + give:
        copy.wait()


def shards(
    grid_latent,
    mesh_latent,
    neighbours,
    edge_bias,
    query_weight,
    key_weight,
    value_weight,
    out_weight,
    norm_gain,
):
    band, width = grid_latent.shape
    count, slots = neighbours.shape
    part = count // 2
    cols = width // LANES
    heads = width // HEAD_DIM
    split = heads // 2
    side = width // 2
    chunks = part * slots // LANES
    piece = part // HALVES
    padded = -(-piece // LANES) * LANES
    far = pl.BlockSpec(memory_space=pltpu.HBM)
    copies = REPLY + 5 * HALVES
    bf16, f32, i32 = jnp.bfloat16, jnp.float32, jnp.int32
    return pl.pallas_call(
        body,
        name="attend",
        out_shape=jax.ShapeDtypeStruct((count, side), bf16),
        in_specs=[far] * 9,
        out_specs=far,
        scratch_shapes=[
            pltpu.VMEM((band * cols, LANES), f32),
            pltpu.VMEM((2, PIECE, width), bf16),
            pltpu.VMEM((GROUP * LANES * cols, LANES), f32),
            pltpu.VMEM((piece * slots, width), bf16),
            pltpu.VMEM((2, width, side), bf16),
            pltpu.VMEM((2, width, side), bf16),
            pltpu.VMEM((2, width, side), bf16),
            pltpu.VMEM((width, width), bf16),
            pltpu.VMEM((side,), bf16),
            pltpu.VMEM((side,), bf16),
            pltpu.VMEM((slots, count), i32),
            pltpu.VMEM((split * slots, count), bf16),
            pltpu.VMEM((3, 2 * chunks, LANES), i32),
            pltpu.VMEM((3, 2, split, chunks, LANES), bf16),
            pltpu.VMEM((3, part, width), bf16),
            pltpu.VMEM((2, chunks, LANES), i32),
            pltpu.SMEM((chunks, LANES), i32),
            pltpu.SMEM((chunks, LANES), i32),
            pltpu.SMEM((chunks, LANES), i32),
            pltpu.VMEM((3, 2, split, chunks, LANES), bf16),
            pltpu.VMEM((heads * chunks, LANES), f32),
            pltpu.VMEM((heads * chunks, LANES), f32),
            pltpu.VMEM((heads, part, width), f32),
            pltpu.VMEM((heads, part, width), f32),
            pltpu.VMEM((heads * piece, LANES), f32),
            pltpu.VMEM((heads * piece, LANES), bf16),
            pltpu.VMEM((heads, piece, width), f32),
            pltpu.VMEM((heads, padded, LANES), f32),
            pltpu.VMEM((HALVES, heads, piece, width), f32),
            pltpu.VMEM((HALVES, heads, piece, LANES), f32),
            pltpu.VMEM((2, HALVES, heads, piece, HEAD_DIM), bf16),
            pltpu.VMEM((2, HALVES, SUB, padded), f32),
            pltpu.VMEM((2, HALVES, heads, piece, HEAD_DIM), bf16),
            pltpu.VMEM((2, HALVES, SUB, padded), f32),
            pltpu.VMEM((HALVES, 2, piece, side), bf16),
            pltpu.SemaphoreType.DMA((2,)),
            pltpu.SemaphoreType.DMA((8,)),
            pltpu.SemaphoreType.DMA((3,)),
            pltpu.SemaphoreType.DMA((copies,)),
            pltpu.SemaphoreType.DMA((copies,)),
        ],
        compiler_params=pltpu.CompilerParams(
            collective_id=0, has_side_effects=True, vmem_limit_bytes=56 * 1024 * 1024
        ),
    )(
        grid_latent, mesh_latent, neighbours.T, edge_bias.T,
        query_weight, key_weight, value_weight, out_weight, norm_gain,
    )


def solution(mesh):
    in_specs = (
        P("lat", None),
        P("lat", None),
        P("lat", None),
        P("lat", "head"),
        P(None, "head"),
        P(None, "head"),
        P(None, "head"),
        P("head", None),
        P("head"),
    )
    out_specs = P("lat", "head")
    return jax.shard_map(shards, mesh=mesh, in_specs=in_specs, out_specs=out_specs, check_vma=False)
```

time: 76.1 us -> 49.2 us (0.65)
  the two profiles are of different devices: /device:TPU:5 before, /device:TPU:21 now
where the time goes in v1:
time: 49.2 us; the launch traced here: 49 us
  Pallas kernels  47.2 us (96%)
  local copies, waits for them, and re-layouts  1.72 us (3%)
    pallas_call x1, Pallas kernels, shards(): pl.pallas_call(body, name='attend', out_shape=jax.ShapeDtypeStruct((count...  47.2 us
    unnamed x1, local copies, waits for them, and re-layouts  1.72 us

profile of v1, /device:TPU:21, one launch (start us, length us, event | category | flops | bytes accessed | tf_op | source)
XLA Modules:
  0.0 49.0 jit_solution(5140716239768056610)
XLA Ops:
  0.0 47.2 %attend.1 = bf16[640,256]{1,0:T(8,128)(2,1)} custom-call(bf16[8192,512]{1,0:T(8,128)(2,1)} %grid_in.1, bf16[640,512]{1,0:T(8,128)(2,1)} %mesh_in.1, s32[16,640]{1,0:T(8,128)} %bitcast.2, bf16[32,640]{1,0:T(8,128)(2,1)} %bitcast.3, bf16[512,256]{1,0:T(8,128)(2,1)} %query_in.1, bf16[512,256]{1,0:T(8,128)(2,1)} %key_in.1, bf16[512,256]{1,0:T(8,128)(2,1)} %value_in.1, ...), custom_call_target="tpu_custom_call" | custom-call | tf_op jit(solution)/shard_map/attend/pallas_call | solution.py:470
  47.2 1.7 %copy.11 = bf16[640,256]{1,0:T(8,128)(2,1)} copy(bf16[640,256]{1,0:T(8,128)(2,1)} %attend.1) | data formatting | bytes 655360

commit v2 on v1

--- a/solution.py
+++ b/solution.py
@@ -15,12 +15,13 @@
 PIECE = 1024
 HALVES = 2
 GROUP = 5
+LEAD = 5
 MIX = 10
 MESH = pl.DeviceIdType.MESH
 
 SHARED = 0
 REQUEST = 6
-REQUEST_COPIES = 4
+REQUEST_COPIES = 5
 REPLY = REQUEST + 2 * REQUEST_COPIES
 
 
@@ -104,11 +105,14 @@
     def request(s):
         at, target = REQUEST + s * REQUEST_COPIES, sides[s][0]
         order = order_send.at[s, pl.ds(me * chunks, chunks)]
+        lead, rest = pl.ds(0, part // LEAD), pl.ds(part // LEAD, part - part // LEAD)
+        mesh_rows = mesh_in.at[pl.ds(me * part, part)]
         return (
-            remote(at, mesh_in.at[pl.ds(me * part, part)], nodes.at[s], (target, me)),
+            remote(at, mesh_rows.at[lead], nodes.at[s, lead], (target, me)),
             remote(at + 1, order, order_land.at[s], (target, me)),
             remote(at + 2, bias_send.at[s, me], bias_land.at[s, me], (target, me)),
             remote(at + 3, bias_send.at[s, other], bias_land.at[s, me], (target, other)),
+            remote(at + 4, mesh_rows.at[rest], nodes.at[s, rest], (target, me)),
         )
 
     def answer(s, half):
@@ -188,7 +192,7 @@
 
     @pl.when(sides[1][1])
     def _():
-        for copy in request(1):
+        for copy in request(1)[1:4]:
             copy.start()
 
     shared[5].start()
@@ -198,25 +202,6 @@
         order_send.at[2, pl.ds(me * chunks, chunks)], order_own, order_sems.at[2]
     )
     keep_order.start()
-
-    pieces = band // PIECE
-    for n in range(pieces):
-        fetch(n).wait()
-
-        def widen(step, carry, n=n):
-            row = pl.multiple_of(step * 32, 32)
-            block = stage[n % 2, pl.ds(row, 32), :].astype(f32)
-            for t in range(4):
-                for c in range(cols):
-                    at = (n * PIECE + row + t * SUB) * cols + c
-                    wide[pl.ds(at, SUB, stride=cols), :] = block[
-                        t * SUB : (t + 1) * SUB, c * LANES : (c + 1) * LANES
-                    ]
-            return carry
-
-        lax.fori_loop(0, PIECE // 32, widen, 0)
-        if n + 2 < pieces:
-            fetch(n + 2).start()
 
     diagonal = iota((SUB, LANES), 1) // slots == iota((SUB, LANES), 0)
     lane = iota((padded, LANES), 1)
@@ -290,7 +275,7 @@
         for h in range(heads):
             mixed_ref[h, block(chunk, SUB), :] = summed[h * SUB : (h + 1) * SUB]
 
-    def run(order, fold_ref, bias_ref, mixed_ref, lse_ref, half):
+    def run(order, fold_ref, bias_ref, mixed_ref, lse_ref, half, then=None):
         base = half * piece_chunks
         for u in range(GROUP):
             gather(order, base + u, u)
@@ -306,6 +291,8 @@
         lax.fori_loop(0, piece_chunks // GROUP - 1, scoring, 0)
         for u in range(GROUP):
             score(fold_ref, base, piece_chunks - GROUP + u, u)
+        if then is not None:
+            then()
 
         def softening(n, carry):
             for u in range(piece_chunks):
@@ -329,28 +316,73 @@
             preferred_element_type=f32,
         )
 
+    def address(s):
+        order = (order_low, order_high)[s]
+        return pltpu.make_async_copy(order_land.at[s], order, order_sems.at[s])
+
     lse[...] = jnp.zeros(lse.shape, f32)
-    for copy in mine[2:]:
-        copy.wait()
-    for copy in shared:
-        copy.wait_recv()
-    keep_bias.wait()
+    pieces = band // PIECE
+    for n in range(pieces):
+        fetch(n).wait()
+
+        def widen(step, carry, n=n):
+            row = pl.multiple_of(step * 32, 32)
+            block = stage[n % 2, pl.ds(row, 32), :].astype(f32)
+            for t in range(4):
+                for c in range(cols):
+                    at = (n * PIECE + row + t * SUB) * cols + c
+                    wide[pl.ds(at, SUB, stride=cols), :] = block[
+                        t * SUB : (t + 1) * SUB, c * LANES : (c + 1) * LANES
+                    ]
+            return carry
+
+        lax.fori_loop(0, PIECE // 32, widen, 0)
+        if n + 2 < pieces:
+            fetch(n + 2).start()
+        if n == pieces // 2:
+            for copy in mine[2:]:
+                copy.wait()
+            for copy in shared:
+                copy.wait_recv()
+            keep_bias.wait()
+            project(2, fold_own, bias_own)
+
+    @pl.when(sides[0][3])
+    def _():
+        request(0)[1].wait_recv()
+        address(0).start()
+
     keep_order.wait()
 
-    project(2, fold_own, bias_own)
-    run(order_own, fold_own, bias_own, mixed_own.at[0], lse_own.at[0], 0)
+    def send_down():
+        @pl.when(sides[1][1])
+        def _():
+            request(1)[0].start()
+            request(1)[4].start()
+
+    run(order_own, fold_own, bias_own, mixed_own.at[0], lse_own.at[0], 0, send_down)
+
+    def arrive(s):
+        address(s).wait()
+        for n in (2, 3, 0, 4):
+            request(s)[n].wait_recv()
+
+    @pl.when(sides[0][3])
+    def _():
+        arrive(0)
+
+    @pl.when(sides[1][3])
+    def _():
+        request(1)[1].wait_recv()
+        address(1).start()
 
     for s, order in enumerate((order_low, order_high)):
         _, sent, _, received = sides[s]
 
         @pl.when(received)
         def _(s=s, order=order):
-            needs = request(s)
-            order_copy = pltpu.make_async_copy(order_land.at[s], order, order_sems.at[s])
-            for copy in needs:
-                copy.wait_recv()
-            order_copy.start()
-            order_copy.wait()
+            if s:
+                arrive(s)
             project(s, fold, bias_rows)
             for half in range(HALVES):
                 run(order, fold, bias_rows, mixed, lse, half)

time: 49.2 us -> 40.7 us (0.83)
  the two profiles are of different devices: /device:TPU:21 before, /device:TPU:5 now
where the time goes in v2:
time: 40.7 us; the launch traced here: 40.2 us
  Pallas kernels  38.4 us (94%)
  local copies, waits for them, and re-layouts  1.72 us (4%)
    pallas_call x1, Pallas kernels, shards(): pl.pallas_call(body, name='attend', out_shape=jax.ShapeDtypeStruct((count...  38.4 us
    unnamed x1, local copies, waits for them, and re-layouts  1.72 us

profile of v2, /device:TPU:5, one launch (start us, length us, event | category | flops | bytes accessed | tf_op | source)
XLA Modules:
  0.0 40.2 jit_solution(12643606363009315010)
XLA Ops:
  0.0 38.4 %attend.1 = bf16[640,256]{1,0:T(8,128)(2,1)} custom-call(bf16[8192,512]{1,0:T(8,128)(2,1)} %grid_in.1, bf16[640,512]{1,0:T(8,128)(2,1)} %mesh_in.1, s32[16,640]{1,0:T(8,128)} %bitcast.2, bf16[32,640]{1,0:T(8,128)(2,1)} %bitcast.3, bf16[512,256]{1,0:T(8,128)(2,1)} %query_in.1, bf16[512,256]{1,0:T(8,128)(2,1)} %key_in.1, bf16[512,256]{1,0:T(8,128)(2,1)} %value_in.1, ...), custom_call_target="tpu_custom_call" | custom-call | tf_op jit(solution)/shard_map/attend/pallas_call | solution.py:502
  38.5 1.7 %copy.11 = bf16[640,256]{1,0:T(8,128)(2,1)} copy(bf16[640,256]{1,0:T(8,128)(2,1)} %attend.1) | data formatting | bytes 655360

commit v3 on v2

--- a/solution.py
+++ b/solution.py
@@ -31,7 +31,7 @@
     wide, stage, picked, rows, query_w, key_w, value_w, out_w, gain_mine, gain_theirs,
     neigh, bias, order_send, bias_send, nodes, order_land, order_own, order_low, order_high,
     bias_land, bias_rows, bias_own, fold, fold_own, scores, weights, mixed, lse,
-    mixed_own, lse_own, partial, partial_lse, reply, reply_lse, normed,
+    mixed_own, lse_own, partial, partial_lse, reply, reply_lse, normed, landed,
     stage_sems, local_sems, order_sems, send_sems, recv_sems,
 ):
     band, width = grid_in.shape
@@ -410,7 +410,7 @@
         jnp.where(me == side_of, gain_mine[...], gain_theirs[...]).reshape(1, side).astype(f32)
         for side_of in range(2)
     ]
-    give, keep = [], []
+    give = []
     for half in range(HALVES):
         for s in range(2):
             @pl.when(sides[s][1])
@@ -450,13 +450,16 @@
         variance = jnp.sum(updated * updated, axis=1, keepdims=True) / width - mean * mean
         result = (updated - mean) * lax.rsqrt(variance + EPSILON)
         for b in range(2):
-            normed[half, b] = (result[:, b * side : (b + 1) * side] * gains[b]).astype(bf16)
-        here = out_ref.at[pl.ds(me * part + half * piece, piece)]
-        at = REPLY + 4 * HALVES + half
-        give.append(remote(at, normed.at[half, other], here, partner))
-        keep.append(pltpu.make_async_copy(normed.at[half, me], here, local_sems.at[1 + half]))
+            block_out = (result[:, b * side : (b + 1) * side] * gains[b]).astype(bf16)
+            normed[half, b] = block_out
+            at = pl.multiple_of(me * part + half * piece, piece)
+            @pl.when(me == b)
+            def _(block_out=block_out, at=at):
+                out_ref[pl.ds(at, piece), :] = block_out
+        give.append(remote(
+            REPLY + 4 * HALVES + half, normed.at[half, other], landed.at[half], partner
+        ))
         give[half].start()
-        keep[half].start()
 
     for copy in shared:
         copy.wait_send()
@@ -471,8 +474,10 @@
             for half in range(HALVES):
                 for copy in answer(s, half):
                     copy.wait_send()
-    for copy in keep + give:
+    for half, copy in enumerate(give):
         copy.wait()
+        at = pl.multiple_of(other * part + half * piece, piece)
+        out_ref[pl.ds(at, piece), :] = landed[half]
 
 
 def shards(
@@ -502,9 +507,9 @@
     return pl.pallas_call(
         body,
         name="attend",
-        out_shape=jax.ShapeDtypeStruct((count, side), bf16),
+        out_shape=pltpu.VMEM((count, side), bf16),
         in_specs=[far] * 9,
-        out_specs=far,
+        out_specs=pl.BlockSpec(memory_space=pltpu.VMEM),
         scratch_shapes=[
             pltpu.VMEM((band * cols, LANES), f32),
             pltpu.VMEM((2, PIECE, width), bf16),
@@ -541,6 +546,7 @@
             pltpu.VMEM((2, HALVES, heads, piece, HEAD_DIM), bf16),
             pltpu.VMEM((2, HALVES, SUB, padded), f32),
             pltpu.VMEM((HALVES, 2, piece, side), bf16),
+            pltpu.VMEM((HALVES, piece, side), bf16),
             pltpu.SemaphoreType.DMA((2,)),
             pltpu.SemaphoreType.DMA((8,)),
             pltpu.SemaphoreType.DMA((3,)),

time: 40.7 us -> 39.6 us (0.973)
  local copies, waits for them, and re-layouts: 1.72 us -> 0.73 us
    unnamed x1, local copies, waits for them, and re-layouts: 1.72 us -> 0.73 us
where the time goes in v3:
time: 39.6 us; the launch traced here: 39.1 us
  Pallas kernels  38.3 us (97%)
  local copies, waits for them, and re-layouts  0.73 us (2%)
    pallas_call x1, Pallas kernels, shards(): pl.pallas_call(body, name='attend', out_shape=pltpu.VMEM((count, side), b...  38.3 us

profile of v3, /device:TPU:5, one launch (start us, length us, event | category | flops | bytes accessed | tf_op | source)
XLA Modules:
  0.0 39.1 jit_solution(4257751873780881901)
XLA Ops:
  0.0 38.3 %attend.1 = bf16[640,256]{1,0:T(8,128)(2,1)S(1)} custom-call(bf16[8192,512]{1,0:T(8,128)(2,1)} %grid_in.1, bf16[640,512]{1,0:T(8,128)(2,1)} %mesh_in.1, s32[16,640]{1,0:T(8,128)} %bitcast.2, bf16[32,640]{1,0:T(8,128)(2,1)} %bitcast.3, bf16[512,256]{1,0:T(8,128)(2,1)} %query_in.1, bf16[512,256]{1,0:T(8,128)(2,1)} %key_in.1, bf16[512,256]{1,0:T(8,128)(2,1)} %value_in.1, ...), custom_call_target="tpu_custom_call" | custom-call | tf_op jit(solution)/shard_map/attend/pallas_call | solution.py:507
  38.3 0.7 %copy.11 = bf16[640,256]{1,0:T(8,128)(2,1)} copy(bf16[640,256]{1,0:T(8,128)(2,1)S(1)} %attend.1) | data formatting | bytes 655360
